TPU v7x, 32 devices: a whole 2x2x4 slice. The times are simulated.
32 devices in a mesh: dp: 4 (over y, x), vocab: 8 (over z, core).
Axes of the slice: x: 2, y: 2, z: 4, core: 2. Of those that a mesh axis runs over, the one named last changes fastest.
Arguments:
- hidden: bfloat16 [512, 8192], P('dp', 'vocab'), may hold values from -20 to 20
- weight: bfloat16 [8192, 4752], P('dp', 'vocab'), may hold values from -0.198873782 to 0.198873782
- targets: int32 [512], P('dp'), may hold values from 0 to 4751
- loss_mask: int32 [512], P('dp'), may hold values 0 or 1
Outputs:
- grad_hidden: bfloat16 [512, 8192], P('dp', 'vocab')
- grad_weight: bfloat16 [8192, 4752], P('dp', 'vocab')
- token_loss: float32 [512], P('dp')
- grad_norm: float32 [], replicated
All inputs are finite; a program needn't handle non-finite values. No bound on the sum of `loss_mask` on one device may be relied on, other than what follows from the above.
Results may differ from a plain program's by a relative error of at most 0.0034.
Values may be sent and summed in bfloat16 or wider, within the bound.
A program may use at most 128 MiB of HBM per device.

v0:
```python
import jax
import jax.numpy as jnp
from jax import lax
from jax.sharding import PartitionSpec as P

loss_scale = 16.0


def on_device(hidden, weight, targets, loss_mask):
    shard_width = weight.shape[1]
    col_offset = lax.axis_index("vocab") * shard_width
    full_hidden = lax.all_gather(hidden, "vocab", axis=1, tiled=True)
    hidden_block = lax.all_to_all(full_hidden, "dp", split_axis=1, concat_axis=0, tiled=True)
    full_weight = lax.all_gather(weight, "dp", axis=0, tiled=True)
    logits = jnp.dot(full_hidden, full_weight, preferred_element_type=jnp.float32)
    row_targets, row_mask = (targets, loss_mask)
    local_col = row_targets - col_offset
    onehot = (lax.broadcasted_iota(jnp.int32, logits.shape, 1) == local_col[:, None]).astype(
        jnp.float32
    )
    target_local = jnp.sum(logits * onehot, axis=1)
    local_top = jnp.max(logits, axis=1)
    row_top = lax.pmax(local_top, "vocab")
    local_sum = jnp.sum(jnp.exp(logits - row_top[:, None]), axis=1)
    exp_sum, target_logit = lax.psum((local_sum, target_local), "vocab")
    log_total = row_top + jnp.log(exp_sum)
    row_keep = row_mask.astype(jnp.float32)
    loss_rows = row_keep * (log_total - target_logit)
    softmax = jnp.exp(logits - log_total[:, None])
    dlogits = (loss_scale * row_keep[:, None] * (softmax - onehot)).astype(jnp.bfloat16)
    dlog_all = lax.all_gather(dlogits, "dp", axis=0, tiled=True)
    hidden_terms = lax.dot_general(
        dlogits, full_weight, (((1,), (1,)), ((), ())), preferred_element_type=jnp.float32
    )
    hidden_grad_full = lax.psum_scatter(hidden_terms, "vocab", scatter_dimension=1, tiled=True)
    weight_grad_full = lax.dot_general(
        hidden_block, dlog_all, (((0,), (0,)), ((), ())), preferred_element_type=jnp.float32
    )
    local_squares = jnp.sum(weight_grad_full * weight_grad_full) + jnp.sum(
        hidden_grad_full * hidden_grad_full
    )
    squares_total = lax.psum(local_squares, ("dp", "vocab"))
    return (
        hidden_grad_full.astype(jnp.bfloat16),
        weight_grad_full.astype(jnp.bfloat16),
        loss_rows,
        jnp.sqrt(squares_total),
    )


def solution(mesh):
    placed = (P("dp", "vocab"), P("dp", "vocab"), P("dp"), P("dp"))
    return jax.shard_map(
        on_device,
        mesh=mesh,
        in_specs=placed,
        out_specs=(P("dp", "vocab"), P("dp", "vocab"), P("dp"), P()),
        check_vma=False,
    )
```

profile of v0, /device:TPU:12, one launch (start us, length us, event | category | flops | bytes accessed | tf_op | source)
XLA Modules:
  0.0 285.6 jit_solution(2477782353101069427)
XLA Ops:
  7.2 0.0 copy-start.2
  7.2 0.0 all-gather.3.cloned.1.call-start
  7.2 1.8 copy.8
  9.0 0.0 all-gather.3.cloned.1.call-update
  9.0 0.0 all-gather.5.cloned.1.call-start
  9.1 0.7 all-gather.5.cloned.1.call-update
  9.8 0.0 reduce-scatter.2.cloned.1.call-start
  9.8 0.0 copy-done.2
  9.9 0.0 copy-start.1
  9.9 30.6 %all-gather.3.cloned.1.call-done = bf16[128,8192]{0,1:T(8,128)(2,1)} async-done(((bf16[128,1024]{0,1:T(8,128)(2,1)}), bf16[128,8192]{0,1:T(8,128)(2,1)}) %all-gather.3.cloned.1.call-update) | async-done | bytes 2097168 | tf_op jit(solution)/shard_map/all_gather | solution.py:12
  40.4 100.8 %all-gather.5.cloned.1.call-done = bf16[8192,594]{0,1:T(8,128)(2,1)} async-done(((bf16[2048,594]{0,1:T(8,128)(2,1)}), bf16[8192,594]{0,1:T(8,128)(2,1)}) %all-gather.5.cloned.1.call-update) | async-done | bytes 9732112 | tf_op jit(solution)/shard_map/all_gather | solution.py:14
  141.2 6.2 %fusion = (f32[128]{0:T(128)S(1)}, f32[128,594]{0,1:T(8,128)S(1)}) fusion(bf16[128,8192]{0,1:T(8,128)(2,1)} %all-gather.3.cloned.1.call-done, bf16[8192,594]{0,1:T(8,128)(2,1)} %all-gather.5.cloned.1.call-done), kind=kOutput, calls=%fused_computation.11 | convolution fusion | flops 1245784192 | bytes 12133888 | tf_op jit(solution)/shard_map/dot_general | solution.py:15
  147.4 12.7 %pmax.7 = f32[128]{0:T(128)S(1)} all-reduce(f32[128]{0:T(128)S(1)} %get-tuple-element.15), channel_id=1, replica_groups=mesh['dp'=4,'vocab'=8] {'vocab'}, use_global_device_ids=true, to_apply=%region_1.0 | all-reduce | flops 128 | bytes 1024 | tf_op jit(solution)/shard_map/pmax | solution.py:23
  160.1 0.1 select_reduce_fusion
  160.2 13.6 %all-reduce = (f32[128]{0:T(128)S(1)}, f32[128]{0:T(128)S(1)}) all-reduce(f32[128]{0:T(128)S(1)} %get-tuple-element.5, f32[128]{0:T(128)S(1)} %get-tuple-element.4), channel_id=1, replica_groups=mesh['dp'=4,'vocab'=8] {'vocab'}, use_global_device_ids=true, to_apply=%region_3.0 | all-reduce | flops 256 | bytes 2048 | tf_op jit(solution)/shard_map/psum | solution.py:25
  173.8 0.0 copy-done.1
  173.8 0.5 subtract_multiply_fusion
  174.3 0.1 multiply_convert_fusion
  174.4 8.0 %fusion.1 = f32[128,8192]{1,0:T(8,128)} fusion(bf16[128,594]{0,1:T(8,128)(2,1)S(1)} %multiply_convert_fusion, bf16[8192,594]{0,1:T(8,128)(2,1)} %all-gather.5.cloned.1.call-done), kind=kOutput, calls=%fused_computation.12 | convolution fusion | flops 1245708288 | bytes 14078464 | tf_op jit(solution)/shard_map/dot_general | solution.py:32
  182.4 0.0 copy-start
  182.4 0.0 reduce-scatter.2.cloned.1.call-update
  182.4 1.6 copy-done
  184.0 28.4 %all_to_all.19 = bf16[128,4,2048]{0,2,1:T(8,128)(2,1)} all-to-all(bf16[128,4,2048]{0,2,1:T(8,128)(2,1)S(1)} %bitcast.11), channel_id=1, replica_groups=mesh['dp'=4,'vocab'=8] {'dp'}, dimensions={1} | all-to-all | bytes 4194304 | tf_op jit(solution)/shard_map/all_to_all | solution.py:13
  212.3 2.9 %copy.9 = bf16[4,128,2048]{2,1,0:T(8,128)(2,1)S(1)} copy(bf16[4,128,2048]{1,2,0:T(8,128)(2,1)} %bitcast.12) | data formatting | bytes 4194304 | tf_op jit(solution)/shard_map/all_to_all | solution.py:13
  215.3 10.0 %all_gather.11 = bf16[512,594]{0,1:T(8,128)(2,1)S(1)} all-gather(bf16[128,594]{0,1:T(8,128)(2,1)S(1)} %multiply_convert_fusion), channel_id=1, replica_groups=mesh['dp'=4,'vocab'=8] {'dp'}, dimensions={0}, use_global_device_ids=true | all-gather | bytes 760320 | tf_op jit(solution)/shard_map/all_gather | solution.py:31
  225.3 3.6 %multiply_reduce_fusion = (f32[]{:T(128)}, bf16[2048,594]{0,1:T(8,128)(2,1)}) fusion(bf16[512,594]{0,1:T(8,128)(2,1)S(1)} %all_gather.11, bf16[512,2048]{1,0:T(8,128)(2,1)S(1)} %bitcast.13), kind=kOutput, calls=%fused_computation | convolution fusion | flops 1249357824 | bytes 5138436 | tf_op jit(solution)/shard_map/dot_general | solution.py:36
  228.9 1.2 reduce-scatter.2.cloned.1.call-done
  230.1 2.6 multiply_reduce_fusion.1
  234.0 43.3 %psum.23 = f32[]{:T(128)} all-reduce(f32[]{:T(128)S(6)} %add.15), channel_id=1, replica_groups=mesh['dp'=4,'vocab'=8] {'dp','vocab'}, use_global_device_ids=true, to_apply=%region_9.0 | all-reduce | flops 1 | bytes 8 | tf_op jit(solution)/shard_map/psum | solution.py:42
  (1 shorter events, 0.0 us)
Async XLA Ops:
  7.2 2.7 copy-start.2
  7.2 33.3 %all-gather.3.cloned.1.call-start = ((), (), s32[]{:S(2)}) async-start(), calls=%async_computation.2 | async-start | bytes 2359296 | tf_op jit(solution)/shard_map/all_gather | solution.py:12
  9.0 132.2 %all-gather.5.cloned.1.call-start = ((), (), s32[]{:S(2)}) async-start(), calls=%async_computation.3 | async-start | bytes 12288000 | tf_op jit(solution)/shard_map/all_gather | solution.py:14
  9.8 220.3 %reduce-scatter.2.cloned.1.call-start = ((), (), s32[]{:S(2)}) async-start(), calls=%async_computation.4 | async-start | bytes 4718592 | tf_op jit(solution)/shard_map/reduce_scatter | solution.py:35
  9.9 163.9 %copy-start.1 = (s32[128]{0:T(128)S(1)}, s32[128]{0:T(128)}, u32[]{:S(2)}) copy-start(s32[128]{0:T(128)} %param.7) | copy-start | bytes 1540
  182.4 1.6 copy-start
Sparse Core Ops, SparseCore 0:
  10.2 30.2 all-gather.2
  42.3 98.8 all-gather.4
  182.5 47.5 reduce-scatter.1
where the time goes:
time: 286 us
  waiting for transfers between devices  133 us (47%)
  blocking collectives  108 us (38%)
  matrix products  17.8 us (6%)
  between operations  17 us (6%)
  local copies, waits for them, and re-layouts  6.31 us (2%)
  other arithmetic  3.29 us (1%)
    all_gather x1, waiting for transfers between devices, on_device(): full_weight = lax.all_gather(weight, 'dp', axis=0, tiled=True)  101 us
    psum x1, blocking collectives, on_device(): squares_total = lax.psum(local_squares, ('dp', 'vocab'))  43.3 us
    all_gather x1, waiting for transfers between devices, on_device(): full_hidden = lax.all_gather(hidden, 'vocab', axis=1, tiled=True)  30.6 us
    all_to_all x1, blocking collectives, on_device(): lax.all_to_all(full_hidden, 'dp', split_axis=1, concat_axis=0, tiled=True)  28.4 us
    psum x1, blocking collectives, on_device(): exp_sum, target_logit = lax.psum((local_sum, target_local), 'vocab')  13.6 us
    pmax x1, blocking collectives, on_device(): row_top = lax.pmax(local_top, 'vocab')  12.7 us
    all_gather x1, blocking collectives, on_device(): dlog_all = lax.all_gather(dlogits, 'dp', axis=0, tiled=True)  10 us
    dot_general x1, matrix products, on_device(): lax.dot_general(dlogits, full_weight, (((1,), (1,)), ((), ())), preferred...  8.01 us
  transfers between devices with their start and end apart: 3, of which 3 were waited for; matrix products, arithmetic and copies ran while one was open for 2% of the time, Pallas kernels for 0%

commit v1 on v0

--- a/solution.py
+++ b/solution.py
@@ -6,11 +6,27 @@
 loss_scale = 16.0
 
 
+def swapped_with_each(array, axis, split, join):
+    ways, here = (lax.axis_size(axis), lax.axis_index(axis))
+    width = array.shape[split] // ways
+    dims = list(array.shape)
+    dims[split] = width
+    height = dims[join]
+    dims[join] = height * ways
+    full = jnp.zeros(dims, array.dtype)
+    for mask in range(ways):
+        part = lax.dynamic_slice_in_dim(array, (here ^ mask) * width, width, axis=split)
+        if mask:
+            part = lax.ppermute(part, axis, [(d, d ^ mask) for d in range(ways)])
+        full = lax.dynamic_update_slice_in_dim(full, part, (here ^ mask) * height, axis=join)
+    return full
+
+
 def on_device(hidden, weight, targets, loss_mask):
     shard_width = weight.shape[1]
     col_offset = lax.axis_index("vocab") * shard_width
     full_hidden = lax.all_gather(hidden, "vocab", axis=1, tiled=True)
-    hidden_block = lax.all_to_all(full_hidden, "dp", split_axis=1, concat_axis=0, tiled=True)
+    hidden_block = swapped_with_each(full_hidden, "dp", 1, 0)
     full_weight = lax.all_gather(weight, "dp", axis=0, tiled=True)
     logits = jnp.dot(full_hidden, full_weight, preferred_element_type=jnp.float32)
     row_targets, row_mask = (targets, loss_mask)

time: 286 us -> 285 us (level)
  blocking collectives: 108 us -> 80.3 us
  waiting for transfers between devices: 133 us -> 155 us
  starting transfers between devices: 0.12 us -> 3.6 us
    all_to_all x1 -> x0, blocking collectives: 28.4 us -> none  [on_device(): lax.all_to_all(full_hidden, 'dp', split_axis=1, concat_axis=0, tiled=True)]
    ppermute x0 -> x3, waiting for transfers between devices: none -> 20 us  [swapped_with_each(): part = lax.ppermute(part, axis, [(d, d ^ mask) for d in range(ways)])]
    ppermute x0 -> x3, starting transfers between devices: none -> 3.49 us  [swapped_with_each(): part = lax.ppermute(part, axis, [(d, d ^ mask) for d in range(ways)])]
    all_to_all x1 -> x0, local copies, waits for them, and re-layouts: 2.94 us -> none  [on_device(): lax.all_to_all(full_hidden, 'dp', split_axis=1, concat_axis=0, tiled=True)]
  transfers between devices with their start and end apart: 3 -> 6, of which waited for: 3 -> 5; matrix products, arithmetic and copies ran while one was open for 2% -> 3% of each run, Pallas kernels for 0% -> 0%
where the time goes in v1:
time: 285 us
  waiting for transfers between devices  155 us (54%)
  blocking collectives  80.3 us (28%)
  matrix products  19.3 us (7%)
  between operations  16.9 us (6%)
  local copies, waits for them, and re-layouts  6.44 us (2%)
  starting transfers between devices  3.6 us (1%)
  other arithmetic  3.29 us (1%)
    all_gather x1, waiting for transfers between devices, on_device(): full_weight = lax.all_gather(weight, 'dp', axis=0, tiled=True)  101 us
    psum x1, blocking collectives, on_device(): squares_total = lax.psum(local_squares, ('dp', 'vocab'))  43.3 us
    all_gather x1, waiting for transfers between devices, on_device(): full_hidden = lax.all_gather(hidden, 'vocab', axis=1, tiled=True)  31.1 us
    ppermute x3, waiting for transfers between devices, swapped_with_each(): part = lax.ppermute(part, axis, [(d, d ^ mask) for d in range(ways)])  20 us
    psum x1, blocking collectives, on_device(): exp_sum, target_logit = lax.psum((local_sum, target_local), 'vocab')  13.6 us
    pmax x1, blocking collectives, on_device(): row_top = lax.pmax(local_top, 'vocab')  12.7 us
    all_gather x1, blocking collectives, on_device(): dlog_all = lax.all_gather(dlogits, 'dp', axis=0, tiled=True)  10.7 us
    dot_general x1, matrix products, on_device(): lax.dot_general(dlogits, full_weight, (((1,), (1,)), ((), ())), preferred...  8.01 us
  transfers between devices with their start and end apart: 6, of which 5 were waited for; matrix products, arithmetic and copies ran while one was open for 3% of the time, Pallas kernels for 0%

profile of v1, /device:TPU:12, one launch (start us, length us, event | category | flops | bytes accessed | tf_op | source)
XLA Modules:
  0.0 285.0 jit_solution(10459876607209172909)
XLA Ops:
  7.2 0.0 copy-start.3
  7.2 0.0 all-gather.3.cloned.1.call-start
  7.2 0.7 all-gather.3.cloned.1.call-update
  7.9 0.0 all-gather.5.cloned.1.call-start
  8.0 0.7 all-gather.5.cloned.1.call-update
  8.7 0.0 reduce-scatter.2.cloned.1.call-start
  8.7 0.0 copy-done.3
  8.7 0.0 copy-start.2
  8.7 31.1 %all-gather.3.cloned.1.call-done = bf16[128,8192]{1,0:T(8,128)(2,1)} async-done(((bf16[128,1024]{1,0:T(8,128)(2,1)}), bf16[128,8192]{1,0:T(8,128)(2,1)}) %all-gather.3.cloned.1.call-update) | async-done | bytes 2097168 | tf_op jit(solution)/shard_map/all_gather | solution.py:28
  39.9 100.8 %all-gather.5.cloned.1.call-done = bf16[8192,594]{0,1:T(8,128)(2,1)} async-done(((bf16[2048,594]{0,1:T(8,128)(2,1)}), bf16[8192,594]{0,1:T(8,128)(2,1)}) %all-gather.5.cloned.1.call-update) | async-done | bytes 9732112 | tf_op jit(solution)/shard_map/all_gather | solution.py:30
  140.6 6.2 %fusion = (f32[128]{0:T(128)S(1)}, f32[128,594]{0,1:T(8,128)S(1)}) fusion(bf16[128,8192]{1,0:T(8,128)(2,1)} %all-gather.3.cloned.1.call-done, bf16[8192,594]{0,1:T(8,128)(2,1)} %all-gather.5.cloned.1.call-done), kind=kOutput, calls=%fused_computation.17 | convolution fusion | flops 1245784192 | bytes 12133888 | tf_op jit(solution)/shard_map/dot_general | solution.py:31
  146.8 12.7 %pmax.7 = f32[128]{0:T(128)S(1)} all-reduce(f32[128]{0:T(128)S(1)} %get-tuple-element.19), channel_id=1, replica_groups=mesh['dp'=4,'vocab'=8] {'vocab'}, use_global_device_ids=true, to_apply=%region_1.0 | all-reduce | flops 128 | bytes 1024 | tf_op jit(solution)/shard_map/pmax | solution.py:39
  159.5 0.1 select_reduce_fusion
  159.6 13.6 %all-reduce = (f32[128]{0:T(128)S(1)}, f32[128]{0:T(128)S(1)}) all-reduce(f32[128]{0:T(128)S(1)} %get-tuple-element.5, f32[128]{0:T(128)S(1)} %get-tuple-element.4), channel_id=1, replica_groups=mesh['dp'=4,'vocab'=8] {'vocab'}, use_global_device_ids=true, to_apply=%region_3.0 | all-reduce | flops 256 | bytes 2048 | tf_op jit(solution)/shard_map/psum | solution.py:41
  173.2 0.0 copy-done.2
  173.2 0.5 subtract_multiply_fusion
  173.7 0.1 multiply_convert_fusion
  173.8 8.0 %fusion.1 = f32[128,8192]{1,0:T(8,128)} fusion(bf16[128,594]{0,1:T(8,128)(2,1)S(1)} %multiply_convert_fusion, bf16[8192,594]{0,1:T(8,128)(2,1)} %all-gather.5.cloned.1.call-done), kind=kOutput, calls=%fused_computation.18 | convolution fusion | flops 1245708288 | bytes 14078464 | tf_op jit(solution)/shard_map/dot_general | solution.py:48
  181.9 0.0 reduce-scatter.2.cloned.1.call-update
  181.9 0.0 copy-start
  181.9 0.2 broadcast_in_dim.2
  182.2 1.3 copy-done
  183.5 1.0 constant_dynamic-slice_fusion
  184.5 0.0 copy-start.1
  184.5 1.3 copy-done.1
  185.8 0.6 collective-permute-start
  186.4 1.5 collective-permute-start.1
  187.9 1.5 collective-permute-start.2
  189.3 11.5 %collective-permute-done = bf16[128,2048]{1,0:T(8,128)(2,1)S(1)} collective-permute-done((bf16[128,2048]{1,0:T(8,128)(2,1)}, bf16[128,2048]{1,0:T(8,128)(2,1)S(1)}, u32[]{:S(2)}, u32[]{:S(2)}) %collective-permute-start) | collective-permute-done | bytes 524320 | tf_op jit(solution)/shard_map/ppermute | solution.py:20
  200.8 0.8 constant_dynamic-update-slice_fusion.1
  201.7 0.0 collective-permute-done.1
  201.7 0.8 constant_dynamic-update-slice_fusion
  202.5 8.5 %collective-permute-done.2 = bf16[128,2048]{1,0:T(8,128)(2,1)S(1)} collective-permute-done((bf16[128,2048]{1,0:T(8,128)(2,1)S(1)}, bf16[128,2048]{1,0:T(8,128)(2,1)S(1)}, u32[]{:S(2)}, u32[]{:S(2)}) %collective-permute-start.2) | collective-permute-done | bytes 524320 | tf_op jit(solution)/shard_map/ppermute | solution.py:20
  211.0 0.8 constant_dynamic-update-slice_fusion.2
  211.9 10.7 %all_gather.11 = bf16[512,594]{0,1:T(8,128)(2,1)S(1)} all-gather(bf16[128,594]{0,1:T(8,128)(2,1)S(1)} %multiply_convert_fusion), channel_id=1, replica_groups=mesh['dp'=4,'vocab'=8] {'dp'}, dimensions={0}, use_global_device_ids=true | all-gather | bytes 760320 | tf_op jit(solution)/shard_map/all_gather | solution.py:47
  222.6 5.1 %multiply_reduce_fusion = (f32[]{:T(128)}, bf16[2048,594]{0,1:T(8,128)(2,1)}) fusion(bf16[512,2048]{1,0:T(8,128)(2,1)} %constant_dynamic-update-slice_fusion.2, bf16[512,594]{0,1:T(8,128)(2,1)S(1)} %all_gather.11), kind=kOutput, calls=%fused_computation | convolution fusion | flops 1249357824 | bytes 5138436 | tf_op jit(solution)/shard_map/dot_general | solution.py:52
  227.7 1.9 reduce-scatter.2.cloned.1.call-done
  229.6 2.6 multiply_reduce_fusion.1
  233.4 43.3 %psum.23 = f32[]{:T(128)} all-reduce(f32[]{:T(128)S(6)} %add.47), channel_id=1, replica_groups=mesh['dp'=4,'vocab'=8] {'dp','vocab'}, use_global_device_ids=true, to_apply=%region_9.0 | all-reduce | flops 1 | bytes 8 | tf_op jit(solution)/shard_map/psum | solution.py:58
  (1 shorter events, 0.0 us)
Async XLA Ops:
  7.2 1.5 copy-start.3
  7.2 32.7 %all-gather.3.cloned.1.call-start = ((), (), s32[]{:S(2)}) async-start(), calls=%async_computation.1 | async-start | bytes 2359296 | tf_op jit(solution)/shard_map/all_gather | solution.py:28
  7.9 132.7 %all-gather.5.cloned.1.call-start = ((), (), s32[]{:S(2)}) async-start(), calls=%async_computation.2 | async-start | bytes 12288000 | tf_op jit(solution)/shard_map/all_gather | solution.py:30
  8.7 220.9 %reduce-scatter.2.cloned.1.call-start = ((), (), s32[]{:S(2)}) async-start(), calls=%async_computation.3 | async-start | bytes 4718592 | tf_op jit(solution)/shard_map/reduce_scatter | solution.py:51
  8.7 164.5 %copy-start.2 = (s32[128]{0:T(128)S(1)}, s32[128]{0:T(128)}, u32[]{:S(2)}) copy-start(s32[128]{0:T(128)} %param.7) | copy-start | bytes 1540
  181.9 1.6 copy-start
  184.5 1.4 copy-start.1
  185.8 15.0 %collective-permute-start = (bf16[128,2048]{1,0:T(8,128)(2,1)}, bf16[128,2048]{1,0:T(8,128)(2,1)S(1)}, u32[]{:S(2)}, u32[]{:S(2)}) collective-permute-start(bf16[128,2048]{1,0:T(8,128)(2,1)} %get-tuple-element.14), channel_id=1, source_target_pairs={{0,8},{8,0},{16,24},{24,16},{1,9},{9,1},{17,25},{25,17},{2,10},{10... | collective-permute-start | bytes 1572872 | tf_op jit(solution)/shard_map/ppermute | solution.py:20
  186.4 15.3 %collective-permute-start.1 = (bf16[128,2048]{1,0:T(8,128)(2,1)S(1)}, bf16[128,2048]{1,0:T(8,128)(2,1)S(1)}, u32[]{:S(2)}, u32[]{:S(2)}) collective-permute-start(bf16[128,2048]{1,0:T(8,128)(2,1)S(1)} %get-tuple-element.13), channel_id=1, source_target_pairs={{0,16},{8,24},{16,0},{24,8},{1,17},{9,25},{17,1},{25,9},{2,18},{10... | collective-permute-start | bytes 1572872 | tf_op jit(solution)/shard_map/ppermute | solution.py:20
  187.9 23.2 %collective-permute-start.2 = (bf16[128,2048]{1,0:T(8,128)(2,1)S(1)}, bf16[128,2048]{1,0:T(8,128)(2,1)S(1)}, u32[]{:S(2)}, u32[]{:S(2)}) collective-permute-start(bf16[128,2048]{1,0:T(8,128)(2,1)S(1)} %get-tuple-element.12), channel_id=1, source_target_pairs={{0,24},{8,16},{16,8},{24,0},{1,25},{9,17},{17,9},{25,1},{2,26},{10... | collective-permute-start | bytes 1572872 | tf_op jit(solution)/shard_map/ppermute | solution.py:20
Sparse Core Ops, SparseCore 0:
  9.6 30.2 all-gather.2
  41.7 98.8 all-gather.4
  182.0 47.5 reduce-scatter.1
